TPU v7x, 32 devices: a whole 2x2x4 slice. The times are simulated.
32 devices in a mesh: fsdp: 4 (over y, x), head: 4 (over z), tensor: 2 (over core).
Axes of the slice: x: 2, y: 2, z: 4, core: 2. Of those that a mesh axis runs over, the one named last changes fastest.
Arguments:
- activations: bfloat16 [2, 16, 197, 768], P(None, ('fsdp', 'head')), may hold values from -6 to 6
- w_qkv: bfloat16 [3, 768, 768], P(None, 'fsdp', 'head'), may hold values from -0.21875 to 0.21875
- w_out: bfloat16 [768, 768], P('head', 'fsdp'), may hold values from -0.875 to 0.875
- gain_one: float32 [768], replicated, may hold values from 0.5 to 1.5
- gain_two: float32 [768], replicated, may hold values from 0.5 to 1.5
- w_router: bfloat16 [768, 8], replicated, may hold values from -0.15625 to 0.15625
- w_in: bfloat16 [8, 768, 3072], P('head', 'fsdp', 'tensor'), may hold values from -0.21875 to 0.21875
- w_down: bfloat16 [8, 3072, 768], P('head', 'tensor', 'fsdp'), may hold values from -0.625 to 0.625
- routes: int32 [2, 16, 197, 2], P(None, ('fsdp', 'head')), may hold values from 0 to 7, as said below
- slot_index: int32 [2, 16, 197, 2], P(None, ('fsdp', 'head')), may hold values from 0 to 63, as said below
- keep_mask: int32 [2, 16, 197, 2], P(None, ('fsdp', 'head')), may hold values from 0 to 1, as said below
- cotangent: bfloat16 [2, 16, 197, 768], P(None, ('fsdp', 'head')), may hold values from -6 to 6
Outputs:
- block_out: bfloat16 [2, 16, 197, 768], P(None, ('fsdp', 'head'))
- grad_input: float32 [2, 16, 197, 768], P(None, ('fsdp', 'head'))
- grad_qkv: float32 [3, 768, 768], P(None, 'fsdp', 'head')
- grad_out: float32 [768, 768], P('head', 'fsdp')
- grad_gain_one: float32 [768], replicated
- grad_gain_two: float32 [768], replicated
- grad_router: float32 [768, 8], replicated
- grad_in: float32 [8, 768, 3072], P('head', 'fsdp', 'tensor')
- grad_down: float32 [8, 3072, 768], P('head', 'tensor', 'fsdp')
Inputs may be any that keep to these rules, and one draw needn't show every extreme that they name: `routes`: the 2 experts of a token differ. In every micro-batch and for every index of fsdp there is an expert that 72 or more rows of each device along head name. `slot_index`: among the kept pairs of one device's rows of one micro-batch that name one expert, slots are distinct. `keep_mask`: of one device's rows of one micro-batch, at most 64 pairs naming one expert are kept, and a pair is dropped only where 64 pairs of that expert are kept; in every micro-batch and index of fsdp some expert has exactly 64 kept pairs from each device along head.
All inputs are finite; a program needn't handle non-finite values.
Results may differ from a plain program's by a relative error of at most 0.02.
Values may be sent and summed in bfloat16 or wider, within the bound.
A program may use at most 192 MiB of HBM per device.

v0:
```python
import jax
import jax.numpy as jnp
from jax import lax
from jax.sharding import PartitionSpec as P

HD = 64
TOP = 2
CAP = 64
highest = lax.Precision.HIGHEST
norm_eps = 1e-06
f32 = jnp.float32
bf16 = jnp.bfloat16


def norm_rows(values, gain_vec):
    centre = values - jnp.mean(values, axis=-1, keepdims=True)
    spread = jnp.mean(centre * centre, axis=-1, keepdims=True)
    return centre * lax.rsqrt(spread + norm_eps) * gain_vec


def gelu_exact(values):
    return jax.nn.gelu(values, approximate=False)


def softmax_last(values):
    return jax.nn.softmax(values, axis=-1)


def ein(spec, left, right):
    return jnp.einsum(spec, left, right, preferred_element_type=f32)


def swap(values):
    return lax.ppermute(values, "tensor", ((0, 1), (1, 0)))


def pick(values):
    return lax.dynamic_index_in_dim(values, lax.axis_index("tensor"), 0, keepdims=False)


def both(mine):
    other = swap(mine)
    first = lax.axis_index("tensor") == 0
    return jnp.stack([jnp.where(first, mine, other), jnp.where(first, other, mine)])


def on_device(
    activations,
    w_qkv,
    w_out,
    gain_one,
    gain_two,
    w_router,
    w_in,
    w_down,
    routes,
    slot_index,
    keep_mask,
    cotangent,
):
    _, img_count, seq_length, width = activations.shape
    groups = lax.axis_size("head")
    local_heads = w_qkv.shape[2] // HD
    local_experts = w_in.shape[0]
    total_experts = local_experts * groups
    slot_count = total_experts * CAP
    tok_rows = img_count * seq_length
    head_scale = HD ** (-0.5)
    qkv_full = lax.all_gather(w_qkv, "fsdp", axis=1, tiled=True)
    out_full = lax.all_gather(w_out, "fsdp", axis=1, tiled=True)
    inputs = pick(activations).astype(f32)
    upstream = pick(cotangent).astype(f32).reshape(tok_rows, width)
    route_rows = pick(routes).reshape(tok_rows, TOP)
    slot_rows = pick(slot_index).reshape(tok_rows, TOP)
    keep_int = pick(keep_mask).reshape(tok_rows, TOP)
    normed, norm_back_one = jax.vjp(norm_rows, inputs, gain_one)
    rows_all = lax.all_gather(normed.astype(bf16), "head", axis=0, tiled=True)
    in_full = lax.all_gather(w_in, "fsdp", axis=1, tiled=True)
    down_full = lax.all_gather(w_down, "fsdp", axis=2, tiled=True)
    image_total = rows_all.shape[0]
    head_shape = (image_total, seq_length, local_heads, HD)
    project = ein("bsd,pde->pbse", rows_all, qkv_full)
    queries = (project[0] * head_scale).astype(bf16).reshape(head_shape)
    key_rows = project[1].astype(bf16).reshape(head_shape)
    value_rows = project[2].astype(bf16).reshape(head_shape)
    scores = ein("bqhd,bkhd->bhqk", queries, key_rows)
    top_score = jnp.max(scores, axis=-1, keepdims=True)
    expo_scores = jnp.exp(scores - top_score)
    row_total = jnp.sum(expo_scores, axis=-1, keepdims=True)
    attn_full = expo_scores / row_total
    attn_low = attn_full.astype(bf16)
    mixed_heads = ein("bhqk,bkhd->bqhd", attn_low, value_rows)
    mixed_heads = mixed_heads.reshape(image_total, seq_length, local_heads * HD).astype(bf16)
    partial_att = ein("bsc,cd->bsd", mixed_heads, out_full)
    attended = lax.psum_scatter(
        partial_att.astype(bf16), "head", scatter_dimension=0, tiled=True
    ).astype(f32)
    hidden = inputs + attended
    normed_two, norm_back_two = jax.vjp(norm_rows, hidden, gain_two)
    token_low = normed_two.astype(bf16).reshape(tok_rows, width)
    logits = jnp.dot(token_low, w_router, preferred_element_type=f32)
    gate_probs, softmax_back = jax.vjp(softmax_last, logits)
    keep_rows = keep_int.astype(f32)
    expert_ids = jnp.arange(total_experts, dtype=jnp.int32)
    slot_ids = jnp.arange(slot_count, dtype=jnp.int32)
    chosen = (route_rows[:, :, None] == expert_ids[None, None, :]).astype(f32)
    gate_values = jnp.sum(gate_probs[:, None, :] * chosen, axis=2) * keep_rows
    flat_slot = route_rows * CAP + slot_rows
    onehot = (
        (flat_slot.T[:, :, None] == slot_ids[None, None, :]) & (keep_int.T[:, :, None] == 1)
    ).astype(bf16)
    weighted = (gate_values.T[:, :, None] * upstream[None, :, :]).astype(bf16)
    tokens_two = jnp.broadcast_to(token_low[None], weighted.shape)
    sent = ein("ktc,ktd->cd", onehot, jnp.concatenate([tokens_two, weighted], axis=-1))
    sent = sent.astype(bf16).reshape(groups, local_experts, CAP, 2 * width)
    mine = lax.all_to_all(sent, "head", split_axis=0, concat_axis=0, tiled=True)
    slots = jnp.stack([mine, swap(mine)])
    received = slots[..., :width]
    slot_grad = slots[..., width:]
    up_proj = ein("mgecd,edf->emgcf", received, in_full)
    active, gelu_back = jax.vjp(gelu_exact, up_proj)
    active = active.astype(bf16)
    partial_out = ein("emgcf,efd->mgecd", active, down_full)
    active_grad = ein("mgecd,efd->emgcf", slot_grad, down_full)
    up_grad = gelu_back(active_grad)[0].astype(bf16)
    partial_in = ein("emgcf,edf->mgecd", up_grad, in_full)
    grad_down = ein("emgcf,mgecd->efd", active, slot_grad)
    grad_in = ein("mgecd,emgcf->edf", received, up_grad)
    partial = jnp.concatenate([partial_out, partial_in], axis=-1)
    back = (partial[0] + swap(partial[1].astype(bf16)).astype(f32)).astype(bf16)
    back = lax.all_to_all(back, "head", split_axis=0, concat_axis=0, tiled=True)
    back = back.reshape(slot_count, 2 * width)
    picked_two = ein("ktc,cd->ktd", onehot, back)
    picked = picked_two[..., :width]
    token_grad = picked_two[0, :, width:] + picked_two[1, :, width:]
    moe_out = jnp.sum(gate_values.T[:, :, None] * picked, axis=0)
    block_out = (hidden + moe_out.reshape(img_count, seq_length, width)).astype(bf16)
    gate_grad = jnp.sum(upstream[None] * picked, axis=-1).T * keep_rows
    prob_grad = jnp.sum(gate_grad[:, :, None] * chosen, axis=1)
    logit_grad = softmax_back(prob_grad)[0]
    grad_router = jnp.dot(token_low.astype(f32).T, logit_grad, precision=highest)
    token_grad = token_grad + jnp.dot(logit_grad, w_router.astype(f32).T, precision=highest)
    hidden_part, grad_gain_two = norm_back_two(token_grad.reshape(img_count, seq_length, width))
    hidden_grad = upstream.reshape(img_count, seq_length, width) + hidden_part
    att_grad_all = lax.all_gather(hidden_grad.astype(bf16), "head", axis=0, tiled=True)
    grad_out = ein("bsc,bsd->cd", mixed_heads, att_grad_all)
    mixed_grad = ein("bsd,cd->bsc", att_grad_all, out_full).astype(bf16).reshape(head_shape)
    value_grad = ein("bhqk,bqhd->bkhd", attn_low, mixed_grad).astype(bf16)
    prob_grads = ein("bqhd,bkhd->bhqk", mixed_grad, value_rows)
    row_delta = jnp.sum(prob_grads * attn_full, axis=-1, keepdims=True)
    score_grad = (attn_full * (prob_grads - row_delta)).astype(bf16)
    query_grad = (ein("bhqk,bkhd->bqhd", score_grad, key_rows) * head_scale).astype(bf16)
    key_grad = ein("bhqk,bqhd->bkhd", score_grad, queries).astype(bf16)
    proj_grad = jnp.stack([query_grad, key_grad, value_grad]).reshape(
        3, image_total, seq_length, local_heads * HD
    )
    row_part = ein("pbse,pde->bsd", proj_grad, qkv_full)
    row_grad = lax.psum_scatter(
        row_part.astype(bf16), "head", scatter_dimension=0, tiled=True
    ).astype(f32)
    grad_qkv = ein("bsd,pbse->pde", rows_all, proj_grad)
    input_part, grad_gain_one = norm_back_one(row_grad)
    input_grad = hidden_grad + input_part

    def owner(part, dim):
        part = lax.psum_scatter(part.astype(bf16), "fsdp", scatter_dimension=dim, tiled=True)
        return part

    def owner_two(part, dim):
        part = owner(part, dim)
        return part.astype(f32) + swap(part).astype(f32)

    small = lax.psum((grad_gain_one, grad_gain_two, grad_router), ("fsdp", "head", "tensor"))
    return (
        both(block_out),
        both(input_grad),
        owner_two(grad_qkv, 1),
        owner_two(grad_out, 1),
        *small,
        owner(grad_in, 1).astype(f32),
        owner(grad_down, 2).astype(f32),
    )


def solution(mesh):
    rows = P(None, ("fsdp", "head"), None, None)
    in_specs = (
        rows,
        P(None, "fsdp", "head"),
        P("head", "fsdp"),
        P(),
        P(),
        P(),
        P("head", "fsdp", "tensor"),
        P("head", "tensor", "fsdp"),
        rows,
        rows,
        rows,
        rows,
    )
    out_specs = (
        rows,
        rows,
        P(None, "fsdp", "head"),
        P("head", "fsdp"),
        P(),
        P(),
        P(),
        P("head", "fsdp", "tensor"),
        P("head", "tensor", "fsdp"),
    )
    return jax.shard_map(
        on_device, mesh=mesh, in_specs=in_specs, out_specs=out_specs, check_vma=False
    )
```

profile of v0, /device:TPU:0, one launch (start us, length us, event | category | flops | bytes accessed | tf_op | source)
XLA Modules:
  0.0 518.0 jit_solution(9751888236601514068)
XLA Ops:
  12.1 19.2 %all_gather.19 = bf16[3,768,192]{2,0,1:T(4,128)(2,1)S(1)} all-gather(bf16[3,192,192]{2,0,1:T(4,128)(2,1)S(1)} %copy.105), channel_id=1, replica_groups=mesh['fsdp'=4,'head'=4,'tensor'=2] {'fsdp'}, dimensions={1}, use_global_device_ids=true | all-gather | bytes 1105920 | tf_op jit(solution)/shard_map/all_gather | solution.py:69
  32.3 10.4 %all_gather.20 = bf16[192,768]{0,1:T(8,128)(2,1)} all-gather(bf16[192,192]{0,1:T(8,128)(2,1)S(1)} %copy.108), channel_id=1, replica_groups=mesh['fsdp'=4,'head'=4,'tensor'=2] {'fsdp'}, dimensions={1}, use_global_device_ids=true | all-gather | bytes 368640 | tf_op jit(solution)/shard_map/all_gather | solution.py:70
  42.7 3.0 all-gather.5.cloned.1.call-done
  59.4 25.5 %reduce-scatter.11.cloned.1.call-done = bf16[1,197,768]{2,1,0:T(8,128)(2,1)} async-done(((bf16[4,197,768]{2,1,0:T(8,128)(2,1)}), bf16[1,197,768]{2,1,0:T(8,128)(2,1)}) %reduce-scatter.11.cloned.1.call-update) | async-done | bytes 302608 | tf_op jit(solution)/shard_map/reduce_scatter | solution.py:95
  91.2 39.7 %all_to_all.10 = bf16[4,2,64,1536]{3,2,1,0:T(8,128)(2,1)S(1)} all-to-all(bf16[4,2,64,1536]{3,2,1,0:T(8,128)(2,1)S(1)} %bitcast.259), channel_id=1, replica_groups=mesh['fsdp'=4,'head'=4,'tensor'=2] {'head'}, dimensions={0} | all-to-all | bytes 3145728 | tf_op jit(solution)/shard_map/all_to_all | solution.py:116
  132.2 3.7 collective-permute-done
  135.9 3.9 pad_maximum_fusion.1
  139.9 7.0 %fusion.33 = (u8[2,2,64,1536]{3,2,1,0:T(8,128)(4,1)S(1)}, u8[2,2,64,1536]{3,2,1,0:T(8,128)(4,1)S(1)}, f32[2,2,4,64,1536]{4,3,2,1,0:T(8,128)S(1)}) fusion(bf16[2,4,2,64,768]{4,3,1,0,2:T(8,128)(2,1)} %get-tuple-element.63, bf16[2,768,1536]{2,1,0:T(8,128)(2,1)} %all-gather.7.cloned.1.call-done), kind=kOutput, calls=%fused_computation.59 | convolution fusion | flops 2435579904 | bytes 13369344 | tf_op jit(solution)/shard_map/mgecd,edf->emgcf/dot_general | solution.py:30
  149.5 15.2 %multiply_convert_fusion = (bf16[2,2,4,64,1536]{4,3,2,1,0:T(8,128)(2,1)}, f32[2,2,4,64,1536]{4,3,2,1,0:T(8,128)}) fusion(f32[2,2,4,64,1536]{4,3,2,1,0:T(8,128)S(1)} %get-tuple-element.79, u8[2,2,64,1536]{3,2,1,0:T(8,128)(4,1)S(1)} %get-tuple-element.46, u8[2,2,64,1536]{3,2,1,0:T(8,128)(4,1)S(1)} %get-tuple-element.45), kind=kLoop, calls=%fused_computation.13 | loop fusion | flops 110100480 | bytes 16515072 | tf_op jit(solution)/shard_map/convert_element_type | solution.py:122
  164.7 23.6 %all-gather.9.cloned.1.call-done = bf16[2,1536,768]{1,2,0:T(8,128)(2,1)} async-done(((bf16[2,1536,192]{1,2,0:T(8,128)(2,1)}), bf16[2,1536,768]{1,2,0:T(8,128)(2,1)}) %all-gather.9.cloned.1.call-update) | async-done | bytes 4718608 | tf_op jit(solution)/shard_map/all_gather | solution.py:79
  188.3 10.4 %add_convert_fusion = bf16[2,2,4,64,1536]{4,3,2,1,0:T(8,128)(2,1)S(1)} fusion(f32[2,2,4,64,1536]{4,3,2,1,0:T(8,128)} %get-tuple-element.59, bf16[2,4,2,64,768]{4,3,1,0,2:T(8,128)(2,1)} %get-tuple-element.62, f32[2,2,4,64,1536]{4,3,2,1,0:T(8,128)} %copy-done.8, bf16[2,1536,768]{1,2,0:T(8,128)(2,1)} %all-gather.9.cloned.1.call-done), kind=kOutput, calls=%fused_computation.12 | convolution fusion | flops 2437939200 | bytes 22020096 | tf_op jit(solution)/shard_map/mgecd,efd->emgcf/dot_general | solution.py:30
  198.7 5.7 %fusion.25 = f32[2,4,2,64,768]{4,3,1,0,2:T(8,128)S(1)} fusion(bf16[2,2,4,64,1536]{4,3,2,1,0:T(8,128)(2,1)S(1)} %add_convert_fusion, bf16[2,768,1536]{2,1,0:T(8,128)(2,1)} %all-gather.7.cloned.1.call-done), kind=kOutput, calls=%fused_computation.50 | convolution fusion | flops 2415919104 | bytes 11010048 | tf_op jit(solution)/shard_map/emgcf,edf->mgecd/dot_general | solution.py:30
  207.4 3.4 collective-permute-done.1
  212.5 4.6 all-to-all-start.1
  217.3 37.2 %all-to-all-done.1 = bf16[4,2,64,1536]{3,2,1,0:T(8,128)(2,1)} async-done(((bf16[4,2,64,1536]{3,2,1,0:T(8,128)(2,1)}), bf16[4,2,64,1536]{3,2,1,0:T(8,128)(2,1)}, u32[]{:S(2)}, u32[]{:S(2)}) %all-to-all-start.1) | async-done | bytes 1572896 | tf_op jit(solution)/shard_map/all_to_all | solution.py:131
  262.0 29.3 %all-gather.11.cloned.1.call-done = bf16[4,197,768]{2,1,0:T(8,128)(2,1)} async-done(((bf16[1,197,768]{2,1,0:T(8,128)(2,1)}), bf16[4,197,768]{2,1,0:T(8,128)(2,1)}) %all-gather.11.cloned.1.call-update) | async-done | bytes 1210384 | tf_op jit(solution)/shard_map/all_gather | solution.py:145
  303.3 3.5 bitcast_convert_fusion.2
  313.0 7.2 %bitcast_convert_fusion.1 = bf16[2,768,1536]{2,1,0:T(8,128)(2,1)} fusion(bf16[2,2,4,64,1536]{4,3,2,1,0:T(8,128)(2,1)} %copy-done.35, bf16[2,4,2,64,768]{4,3,1,0,2:T(8,128)(2,1)} %get-tuple-element.63), kind=kOutput, calls=%fused_computation.3 | convolution fusion | flops 2418278400 | bytes 9437184 | tf_op jit(solution)/shard_map/mgecd,emgcf->edf/dot_general | solution.py:30
  321.6 6.3 %bitcast_convert_fusion = bf16[2,1536,768]{1,2,0:T(8,128)(2,1)} fusion(bf16[2,2,4,64,1536]{4,3,2,1,0:T(8,128)(2,1)} %get-tuple-element.58, bf16[2,4,2,64,768]{4,3,1,0,2:T(8,128)(2,1)S(1)} %copy-done.19), kind=kOutput, calls=%fused_computation.2 | convolution fusion | flops 2418278400 | bytes 9437184 | tf_op jit(solution)/shard_map/emgcf,mgecd->efd/dot_general | solution.py:30
  331.8 26.3 %reduce-scatter.13.cloned.1.call-done = bf16[1,197,768]{2,1,0:T(8,128)(2,1)} async-done(((bf16[4,197,768]{2,1,0:T(8,128)(2,1)}), bf16[1,197,768]{2,1,0:T(8,128)(2,1)}) %reduce-scatter.13.cloned.1.call-update) | async-done | bytes 302608 | tf_op jit(solution)/shard_map/reduce_scatter | solution.py:158
  364.8 22.8 %reduce-scatter.19.cloned.1.call-done = bf16[192,576]{1,0:T(8,128)(2,1)} async-done(((bf16[768,576]{1,0:T(8,128)(2,1)}), bf16[192,576]{1,0:T(8,128)(2,1)}) %reduce-scatter.19.cloned.1.call-update) | async-done | bytes 221200
  391.8 40.7 %all-reduce = (f32[768]{0:T(1024)}, f32[768]{0:T(1024)}, f32[768,8]{0,1:T(8,128)}) all-reduce(f32[768]{0:T(1024)S(1)} %get-tuple-element.51, f32[768]{0:T(1024)S(1)} %get-tuple-element.49, f32[768,8]{0,1:T(8,128)S(1)} %fusion.91), channel_id=1, replica_groups=mesh['fsdp'=4,'head'=4,'tensor'=2] {'fsdp','head','tensor'}, use_global_device_ids=true, to_apply=%region_23.24 | all-reduce | flops 7680 | bytes 61440 | tf_op jit(solution)/shard_map/psum | solution.py:173
  435.0 13.0 %reduce-scatter.15.cloned.1.call-done = bf16[2,192,1536]{2,1,0:T(8,128)(2,1)} async-done(((bf16[2,768,1536]{2,1,0:T(8,128)(2,1)}), bf16[2,192,1536]{2,1,0:T(8,128)(2,1)}) %reduce-scatter.15.cloned.1.call-update) | async-done | bytes 1179664 | tf_op jit(solution)/shard_map/reduce_scatter | solution.py:166
  450.9 56.8 %reduce-scatter.17.cloned.1.call-done = bf16[2,1536,192]{1,2,0:T(8,128)(2,1)} async-done(((bf16[2,1536,768]{1,2,0:T(8,128)(2,1)}), bf16[2,1536,192]{1,2,0:T(8,128)(2,1)}) %reduce-scatter.17.cloned.1.call-update) | async-done | bytes 1179664 | tf_op jit(solution)/shard_map/reduce_scatter | solution.py:166
  (186 shorter events, 83.4 us)
Async XLA Ops:
  8.0 37.7 %all-gather.5.cloned.1.call-start = ((), (), s32[]{:S(2)}) async-start(), calls=%async_computation.8 | async-start | bytes 1536000 | tf_op jit(solution)/shard_map/all_gather | solution.py:77
  11.7 73.2 %reduce-scatter.11.cloned.1.call-start = ((), (), s32[]{:S(2)}) async-start(), calls=%async_computation.9 | async-start | bytes 1536000 | tf_op jit(solution)/shard_map/reduce_scatter | solution.py:95
  51.2 243.5 %copy-start.2 = (f32[4,3,197,197]{2,3,1,0:T(8,128)}, f32[4,3,197,197]{2,3,1,0:T(8,128)S(1)}, u32[]{:S(2)}) copy-start(f32[4,3,197,197]{2,3,1,0:T(8,128)S(1)} %get-tuple-element.76) | copy-start | bytes 5588500
  55.3 32.0 %copy-start.29 = (f32[768]{0:T(1024)S(1)}, f32[768]{0:T(1024)}, u32[]{:S(2)}) copy-start(f32[768]{0:T(1024)} %param.16) | copy-start | bytes 9220
  55.3 33.1 %copy-start.30 = (bf16[768,8]{0,1:T(8,128)(2,1)S(1)}, bf16[768,8]{0,1:T(8,128)(2,1)}, u32[]{:S(2)}) copy-start(bf16[768,8]{0,1:T(8,128)(2,1)} %param.17) | copy-start | bytes 36868
  55.3 84.6 %all-gather.7.cloned.1.call-start = ((), (), s32[]{:S(2)}) async-start(), calls=%async_computation.10 | async-start | bytes 5898240 | tf_op jit(solution)/shard_map/all_gather | solution.py:78
  55.9 132.4 %all-gather.9.cloned.1.call-start = ((), (), s32[]{:S(2)}) async-start(), calls=%async_computation.11 | async-start | bytes 5898240 | tf_op jit(solution)/shard_map/all_gather | solution.py:79
  132.2 3.8 collective-permute-start
  207.4 3.5 collective-permute-start.1
  212.5 42.0 %all-to-all-start.1 = ((bf16[4,2,64,1536]{3,2,1,0:T(8,128)(2,1)}), bf16[4,2,64,1536]{3,2,1,0:T(8,128)(2,1)}, u32[]{:S(2)}, u32[]{:S(2)}) async-start(bf16[4,2,64,1536]{3,2,1,0:T(8,128)(2,1)} %copy.114), calls=%async_computation.2 | async-start | bytes 3145728 | tf_op jit(solution)/shard_map/all_to_all | solution.py:131
  217.1 74.2 %all-gather.11.cloned.1.call-start = ((), (), s32[]{:S(2)}) async-start(), calls=%async_computation.12 | async-start | bytes 1536000 | tf_op jit(solution)/shard_map/all_gather | solution.py:145
  258.4 32.9 %copy-start.17 = (bf16[192,768]{0,1:T(8,128)(2,1)S(1)}, bf16[192,768]{0,1:T(8,128)(2,1)}, u32[]{:S(2)}) copy-start(bf16[192,768]{0,1:T(8,128)(2,1)} %all_gather.20) | copy-start | bytes 884740
  261.9 68.7 %reduce-scatter.21.cloned.1.call-start = ((), (), s32[]{:S(2)}) async-start(), calls=%async_computation.17 | async-start | bytes 491520
  300.9 57.1 %reduce-scatter.13.cloned.1.call-start = ((), (), s32[]{:S(2)}) async-start(), calls=%async_computation.13 | async-start | bytes 1536000 | tf_op jit(solution)/shard_map/reduce_scatter | solution.py:158
  306.8 80.8 %reduce-scatter.19.cloned.1.call-start = ((), (), s32[]{:S(2)}) async-start(), calls=%async_computation.16 | async-start | bytes 1228800
  313.0 135.0 %reduce-scatter.15.cloned.1.call-start = ((), (), s32[]{:S(2)}) async-start(), calls=%async_computation.14 | async-start | bytes 5898240 | tf_op jit(solution)/shard_map/reduce_scatter | solution.py:166
  320.2 187.5 %reduce-scatter.17.cloned.1.call-start = ((), (), s32[]{:S(2)}) async-start(), calls=%async_computation.15 | async-start | bytes 5898240 | tf_op jit(solution)/shard_map/reduce_scatter | solution.py:166
  327.9 32.8 %copy-start.5 = (bf16[1,1,197,768]{3,0,2,1:T(2,128)(2,1)S(1)}, bf16[1,1,197,768]{3,0,2,1:T(2,128)(2,1)}, u32[]{:S(2)}) copy-start(bf16[1,1,197,768]{3,0,2,1:T(2,128)(2,1)} %copy-done.3) | copy-start | bytes 907780
  327.9 32.8 %copy-start.10 = (f32[1,197,768]{2,1,0:T(8,128)S(1)}, f32[1,197,768]{2,1,0:T(8,128)}, u32[]{:S(2)}) copy-start(f32[1,197,768]{2,1,0:T(8,128)} %copy-done.9) | copy-start | bytes 1815556
  328.9 1.6 collective-permute-start.2
  331.6 57.5 %collective-permute-start.5 = (bf16[192,192]{1,0:T(8,128)(2,1)S(1)}, bf16[192,192]{1,0:T(8,128)(2,1)S(1)}, u32[]{:S(2)}, u32[]{:S(2)}) collective-permute-start(bf16[192,192]{1,0:T(8,128)(2,1)S(1)} %copy.150), channel_id=1, source_target_pairs={{0,1},{1,0},{2,3},{3,2},{4,5},{5,4},{6,7},{7,6},{8,9},{9,8},{10,11... | collective-permute-start | bytes 221192 | tf_op jit(solution)/shard_map/ppermute | solution.py:34
  363.4 69.0 %collective-permute-start.3 = (f32[1,197,768]{2,0,1:T(1,128)}, f32[1,197,768]{2,0,1:T(1,128)S(1)}, u32[]{:S(2)}, u32[]{:S(2)}) collective-permute-start(f32[1,197,768]{2,0,1:T(1,128)} %copy.123), channel_id=1, source_target_pairs={{0,1},{1,0},{2,3},{3,2},{4,5},{5,4},{6,7},{7,6},{8,9},{9,8},{10,11... | collective-permute-start | bytes 1815560 | tf_op jit(solution)/shard_map/ppermute | solution.py:34
  389.0 1.6 collective-permute-start.4
  432.7 78.0 %copy-start.1 = (bf16[2,1,197,768]{3,0,2,1:T(2,128)(2,1)S(1)}, bf16[2,1,197,768]{3,0,2,1:T(2,128)(2,1)}, u32[]{:S(2)}) copy-start(bf16[2,1,197,768]{3,0,2,1:T(2,128)(2,1)} %param.12) | copy-start | bytes 1815556
  (29 other events, 143.6 us)
Sparse Core Ops, SparseCore 0:
  11.9 33.8 all-gather.4
  55.4 29.4 reduce-scatter.10
  262.0 29.2 all-gather.10
Sparse Core Ops, SparseCore 1:
  57.7 56.0 all-gather.6
  132.3 55.9 all-gather.8
  301.0 23.8 reduce-scatter.20
  327.8 30.2 reduce-scatter.12
  361.6 25.9 reduce-scatter.18
  390.6 57.3 reduce-scatter.14
  450.8 56.8 reduce-scatter.16
where the time goes:
time: 525 us; the launch traced here: 518 us
  waiting for transfers between devices  247 us (47%)
  blocking collectives  110 us (21%)
  matrix products  65.6 us (12%)
  other arithmetic  44.1 us (8%)
  local copies, waits for them, and re-layouts  28.8 us (5%)
  between operations  16.2 us (3%)
  starting transfers between devices  5.72 us (1%)
    reduce_scatter x2, waiting for transfers between devices, owner(): lax.psum_scatter(part.astype(bf16), 'fsdp', scatter_dimension=dim, tiled=...  69.8 us
    dot_general x19, matrix products, ein(): return jnp.einsum(spec, left, right, preferred_element_type=f32)  62.4 us
    psum x1, blocking collectives, on_device(): lax.psum((grad_gain_one, grad_gain_two, grad_router), ('fsdp', 'head', 't...  40.7 us
    all_to_all x1, blocking collectives, on_device(): mine = lax.all_to_all(sent, 'head', split_axis=0, concat_axis=0, tiled=True)  39.7 us
    all_to_all x1, waiting for transfers between devices, on_device(): back = lax.all_to_all(back, 'head', split_axis=0, concat_axis=0, tiled=True)  37.2 us
    all_gather x1, waiting for transfers between devices, on_device(): lax.all_gather(hidden_grad.astype(bf16), 'head', axis=0, tiled=True)  29.3 us
    reduce_scatter x1, waiting for transfers between devices, on_device(): lax.psum_scatter(row_part.astype(bf16), 'head', scatter_dimension=0, tile...  26.3 us
    reduce_scatter x1, waiting for transfers between devices, on_device(): lax.psum_scatter(partial_att.astype(bf16), 'head', scatter_dimension=0, t...  25.5 us
  transfers between devices with their start and end apart: 17, of which 13 were waited for; matrix products, arithmetic and copies ran while one was open for 15% of the time, Pallas kernels for 0%

commit v1 on v0

--- a/solution.py
+++ b/solution.py
@@ -10,6 +10,24 @@
 norm_eps = 1e-06
 f32 = jnp.float32
 bf16 = jnp.bfloat16
+
+
+def ring_gather(array, axis, dim):
+    ways, here, step = (lax.axis_size(axis), lax.axis_index(axis), array.shape[dim])
+    lengths = [n * ways if d == dim else n for d, n in enumerate(array.shape)]
+    full = lax.dynamic_update_slice_in_dim(
+        jnp.zeros(lengths, array.dtype), array, here * step, axis=dim
+    )
+    going_up = going_down = array
+    for far in range(1, ways // 2 + 1):
+        going_up = lax.ppermute(going_up, axis, [(d, (d + 1) % ways) for d in range(ways)])
+        full = lax.dynamic_update_slice_in_dim(full, going_up, (here - far) % ways * step, axis=dim)
+        if 2 * far < ways:
+            going_down = lax.ppermute(going_down, axis, [(d, (d - 1) % ways) for d in range(ways)])
+            full = lax.dynamic_update_slice_in_dim(
+                full, going_down, (here + far) % ways * step, axis=dim
+            )
+    return full
 
 
 def norm_rows(values, gain_vec):
@@ -76,7 +94,7 @@
     normed, norm_back_one = jax.vjp(norm_rows, inputs, gain_one)
     rows_all = lax.all_gather(normed.astype(bf16), "head", axis=0, tiled=True)
     in_full = lax.all_gather(w_in, "fsdp", axis=1, tiled=True)
-    down_full = lax.all_gather(w_down, "fsdp", axis=2, tiled=True)
+    down_full = ring_gather(w_down, "fsdp", 2)
     image_total = rows_all.shape[0]
     head_shape = (image_total, seq_length, local_heads, HD)
     project = ein("bsd,pde->pbse", rows_all, qkv_full)

time: 525 us -> 580 us (1.10)
  local copies, waits for them, and re-layouts: 28.8 us -> 104 us
  blocking collectives: 110 us -> 70.3 us
  waiting for transfers between devices: 247 us -> 258 us
  starting transfers between devices: 5.72 us -> 14.8 us
    dynamic_update_slice x0 -> x4, local copies, waits for them, and re-layouts: none -> 64.5 us  [the longest x2 31.8 us: ring_gather(): lax.dynamic_update_slice_in_dim(full, going_up, (here - far) % ways * ste...]
    all_to_all x1 -> x0, blocking collectives: 39.7 us -> none  [on_device(): mine = lax.all_to_all(sent, 'head', split_axis=0, concat_axis=0, tiled=True)]
    all_to_all x0 -> x1, waiting for transfers between devices: none -> 35.4 us  [on_device(): mine = lax.all_to_all(sent, 'head', split_axis=0, concat_axis=0, tiled=True)]
    all_gather x1 -> x0, waiting for transfers between devices: 23.6 us -> none  [on_device(): down_full = lax.all_gather(w_down, 'fsdp', axis=2, tiled=True)]
    ppermute x0 -> x3, local copies, waits for them, and re-layouts: none -> 7.51 us  [the longest x2 5.01 us: ring_gather(): lax.ppermute(going_up, axis, [(d, (d + 1) % ways) for d in range(ways)])]
    unnamed x12 -> x11, waiting for transfers between devices: 23.5 us -> 24.2 us
    unnamed x83 -> x80, local copies, waits for them, and re-layouts: 20.7 us -> 20.6 us
  transfers between devices with their start and end apart: 17 -> 20, of which waited for: 13 -> 12; matrix products, arithmetic and copies ran while one was open for 15% -> 24% of each run, Pallas kernels for 0% -> 0%
where the time goes in v1:
time: 580 us; the launch traced here: 571 us
  waiting for transfers between devices  258 us (44%)
  local copies, waits for them, and re-layouts  104 us (18%)
  blocking collectives  70.3 us (12%)
  matrix products  62.9 us (11%)
  other arithmetic  44.5 us (8%)
  between operations  16.3 us (3%)
  starting transfers between devices  14.8 us (3%)
    reduce_scatter x2, waiting for transfers between devices, owner(): lax.psum_scatter(part.astype(bf16), 'fsdp', scatter_dimension=dim, tiled=...  69.8 us
    dot_general x19, matrix products, ein(): return jnp.einsum(spec, left, right, preferred_element_type=f32)  59.8 us
    psum x1, blocking collectives, on_device(): lax.psum((grad_gain_one, grad_gain_two, grad_router), ('fsdp', 'head', 't...  40.7 us
    all_to_all x1, waiting for transfers between devices, on_device(): back = lax.all_to_all(back, 'head', split_axis=0, concat_axis=0, tiled=True)  37.4 us
    all_to_all x1, waiting for transfers between devices, on_device(): mine = lax.all_to_all(sent, 'head', split_axis=0, concat_axis=0, tiled=True)  35.4 us
    dynamic_update_slice x2, local copies, waits for them, and re-layouts, ring_gather(): lax.dynamic_update_slice_in_dim(full, going_up, (here - far) % ways * ste...  31.8 us
    all_gather x1, waiting for transfers between devices, on_device(): lax.all_gather(hidden_grad.astype(bf16), 'head', axis=0, tiled=True)  30.7 us
    reduce_scatter x1, waiting for transfers between devices, on_device(): lax.psum_scatter(partial_att.astype(bf16), 'head', scatter_dimension=0, t...  26.3 us
  transfers between devices with their start and end apart: 20, of which 12 were waited for; matrix products, arithmetic and copies ran while one was open for 24% of the time, Pallas kernels for 0%

profile of v1, /device:TPU:0, one launch (start us, length us, event | category | flops | bytes accessed | tf_op | source)
XLA Modules:
  0.0 570.7 jit_solution(12804070901484625287)
XLA Ops:
  12.2 19.2 %all_gather.16 = bf16[3,768,192]{2,0,1:T(4,128)(2,1)S(1)} all-gather(bf16[3,192,192]{2,0,1:T(4,128)(2,1)S(1)} %copy.117), channel_id=1, replica_groups=mesh['fsdp'=4,'head'=4,'tensor'=2] {'fsdp'}, dimensions={1}, use_global_device_ids=true | all-gather | bytes 1105920 | tf_op jit(solution)/shard_map/all_gather | solution.py:87
  32.3 10.4 %all_gather.17 = bf16[192,768]{0,1:T(8,128)(2,1)} all-gather(bf16[192,192]{0,1:T(8,128)(2,1)S(1)} %copy.120), channel_id=1, replica_groups=mesh['fsdp'=4,'head'=4,'tensor'=2] {'fsdp'}, dimensions={1}, use_global_device_ids=true | all-gather | bytes 368640 | tf_op jit(solution)/shard_map/all_gather | solution.py:88
  58.8 26.3 %reduce-scatter.11.cloned.1.call-done = bf16[1,197,768]{2,1,0:T(8,128)(2,1)} async-done(((bf16[4,197,768]{2,1,0:T(8,128)(2,1)}), bf16[1,197,768]{2,1,0:T(8,128)(2,1)}) %reduce-scatter.11.cloned.1.call-update) | async-done | bytes 302608 | tf_op jit(solution)/shard_map/reduce_scatter | solution.py:113
  92.6 4.4 all-to-all-start
  98.5 35.4 %all-to-all-done = bf16[4,2,64,1536]{3,2,1,0:T(8,128)(2,1)} async-done(((bf16[4,2,64,1536]{3,2,1,0:T(8,128)(2,1)}), bf16[4,2,64,1536]{3,2,1,0:T(8,128)(2,1)}, u32[]{:S(2)}, u32[]{:S(2)}) %all-to-all-start) | async-done | bytes 1572896 | tf_op jit(solution)/shard_map/all_to_all | solution.py:134
  145.5 15.3 %dynamic_update_slice.12 = bf16[2,1536,768]{2,1,0:T(8,128)(2,1)} dynamic-update-slice(bf16[2,1536,768]{2,1,0:T(8,128)(2,1)} %broadcast_in_dim.16, bf16[2,1536,192]{2,1,0:T(8,128)(2,1)} %copy.122, s32[]{:T(128)} %constant.50.clone.1, s32[]{:T(128)} %constant.50.clone.1, s32[]{:T(128)S(6)} %select_n.60) | dynamic-update-slice | bytes 2359300 | tf_op jit(solution)/shard_map/dynamic_update_slice | solution.py:18
  163.3 16.7 %dynamic_update_slice.13 = bf16[2,1536,768]{2,1,0:T(8,128)(2,1)} dynamic-update-slice(bf16[2,1536,768]{2,1,0:T(8,128)(2,1)} %dynamic_update_slice.12, bf16[2,1536,192]{2,1,0:T(8,128)(2,1)} %copy.123, s32[]{:T(128)} %constant.50.clone.1, s32[]{:T(128)} %constant.50.clone.1, s32[]{:T(128)S(6)} %select_n.62) | dynamic-update-slice | bytes 2359300 | tf_op jit(solution)/shard_map/dynamic_update_slice | solution.py:24
  182.5 17.4 %dynamic_update_slice.14 = bf16[2,1536,768]{2,1,0:T(8,128)(2,1)} dynamic-update-slice(bf16[2,1536,768]{2,1,0:T(8,128)(2,1)} %dynamic_update_slice.13, bf16[2,1536,192]{2,1,0:T(8,128)(2,1)} %copy.124, s32[]{:T(128)} %constant.50.clone.1, s32[]{:T(128)} %constant.50.clone.1, s32[]{:T(128)S(6)} %select_n.64) | dynamic-update-slice | bytes 2359300 | tf_op jit(solution)/shard_map/dynamic_update_slice | solution.py:27
  202.4 15.1 %dynamic_update_slice.15 = bf16[2,1536,768]{2,1,0:T(8,128)(2,1)} dynamic-update-slice(bf16[2,1536,768]{2,1,0:T(8,128)(2,1)} %dynamic_update_slice.14, bf16[2,1536,192]{2,1,0:T(8,128)(2,1)} %copy.125, s32[]{:T(128)} %constant.50.clone.1, s32[]{:T(128)} %constant.50.clone.1, s32[]{:T(128)S(6)} %select_n.66) | dynamic-update-slice | bytes 2359300 | tf_op jit(solution)/shard_map/dynamic_update_slice | solution.py:24
  217.6 3.9 pad_maximum_fusion.1
  221.4 6.6 %fusion.33 = (u8[2,2,64,1536]{3,2,1,0:T(8,128)(4,1)S(1)}, u8[2,2,64,1536]{3,2,1,0:T(8,128)(4,1)S(1)}, f32[2,2,4,64,1536]{4,3,2,1,0:T(8,128)S(1)}) fusion(bf16[2,4,2,64,768]{4,3,1,0,2:T(8,128)(2,1)} %get-tuple-element.63, bf16[2,768,1536]{2,1,0:T(8,128)(2,1)} %all-gather.6.cloned.1.call-done), kind=kOutput, calls=%fused_computation.59 | convolution fusion | flops 2435579904 | bytes 13369344 | tf_op jit(solution)/shard_map/mgecd,edf->emgcf/dot_general | solution.py:48
  228.1 15.1 %multiply_convert_fusion = (bf16[2,2,4,64,1536]{4,3,2,1,0:T(8,128)(2,1)S(1)}, f32[2,2,4,64,1536]{4,3,2,1,0:T(8,128)}) fusion(f32[2,2,4,64,1536]{4,3,2,1,0:T(8,128)S(1)} %get-tuple-element.79, u8[2,2,64,1536]{3,2,1,0:T(8,128)(4,1)S(1)} %get-tuple-element.46, u8[2,2,64,1536]{3,2,1,0:T(8,128)(4,1)S(1)} %get-tuple-element.45), kind=kLoop, calls=%fused_computation.13 | loop fusion | flops 110100480 | bytes 16515072 | tf_op jit(solution)/shard_map/convert_element_type | solution.py:140
  245.8 8.6 %add_convert_fusion = bf16[2,2,4,64,1536]{4,3,2,1,0:T(8,128)(2,1)} fusion(f32[2,2,4,64,1536]{4,3,2,1,0:T(8,128)} %get-tuple-element.59, bf16[2,4,2,64,768]{4,3,1,0,2:T(8,128)(2,1)S(1)} %copy-done.16, f32[2,2,4,64,1536]{4,3,2,1,0:T(8,128)S(1)} %get-tuple-element.79, bf16[2,1536,768]{2,1,0:T(8,128)(2,1)} %dynamic_update_slice.15), kind=kOutput, calls=%fused_computation.12 | convolution fusion | flops 2437939200 | bytes 22020096 | tf_op jit(solution)/shard_map/mgecd,efd->emgcf/dot_general | solution.py:48
  254.4 5.9 %fusion.25 = f32[2,4,2,64,768]{4,3,1,0,2:T(8,128)S(1)} fusion(bf16[2,2,4,64,1536]{4,3,2,1,0:T(8,128)(2,1)} %add_convert_fusion, bf16[2,768,1536]{2,1,0:T(8,128)(2,1)} %all-gather.6.cloned.1.call-done), kind=kOutput, calls=%fused_computation.50 | convolution fusion | flops 2415919104 | bytes 11010048 | tf_op jit(solution)/shard_map/emgcf,edf->mgecd/dot_general | solution.py:48
  265.7 5.2 all-to-all-start.1
  270.9 37.4 %all-to-all-done.1 = bf16[4,2,64,1536]{3,2,1,0:T(8,128)(2,1)} async-done(((bf16[4,2,64,1536]{3,2,1,0:T(8,128)(2,1)}), bf16[4,2,64,1536]{3,2,1,0:T(8,128)(2,1)}, u32[]{:S(2)}, u32[]{:S(2)}) %all-to-all-start.1) | async-done | bytes 1572896 | tf_op jit(solution)/shard_map/all_to_all | solution.py:149
  314.5 30.7 %all-gather.8.cloned.1.call-done = bf16[4,197,768]{2,1,0:T(8,128)(2,1)} async-done(((bf16[1,197,768]{2,1,0:T(8,128)(2,1)}), bf16[4,197,768]{2,1,0:T(8,128)(2,1)}) %all-gather.8.cloned.1.call-update) | async-done | bytes 1210384 | tf_op jit(solution)/shard_map/all_gather | solution.py:163
  366.4 7.2 %bitcast_convert_fusion.1 = bf16[2,768,1536]{2,1,0:T(8,128)(2,1)} fusion(bf16[2,2,4,64,1536]{4,3,2,1,0:T(8,128)(2,1)} %add_convert_fusion, bf16[2,4,2,64,768]{4,3,1,0,2:T(8,128)(2,1)} %get-tuple-element.63), kind=kOutput, calls=%fused_computation.3 | convolution fusion | flops 2418278400 | bytes 9437184 | tf_op jit(solution)/shard_map/mgecd,emgcf->edf/dot_general | solution.py:48
  375.0 6.3 %bitcast_convert_fusion = bf16[2,1536,768]{1,2,0:T(8,128)(2,1)} fusion(bf16[2,2,4,64,1536]{4,3,2,1,0:T(8,128)(2,1)} %copy-done.15, bf16[2,4,2,64,768]{4,3,1,0,2:T(8,128)(2,1)S(1)} %copy-done.17), kind=kOutput, calls=%fused_computation.2 | convolution fusion | flops 2418278400 | bytes 9437184 | tf_op jit(solution)/shard_map/emgcf,mgecd->efd/dot_general | solution.py:48
  385.1 25.5 %reduce-scatter.13.cloned.1.call-done = bf16[1,197,768]{2,1,0:T(8,128)(2,1)} async-done(((bf16[4,197,768]{2,1,0:T(8,128)(2,1)}), bf16[1,197,768]{2,1,0:T(8,128)(2,1)}) %reduce-scatter.13.cloned.1.call-update) | async-done | bytes 302608 | tf_op jit(solution)/shard_map/reduce_scatter | solution.py:176
  416.6 23.5 %reduce-scatter.19.cloned.1.call-done = bf16[192,576]{1,0:T(8,128)(2,1)} async-done(((bf16[768,576]{1,0:T(8,128)(2,1)}), bf16[192,576]{1,0:T(8,128)(2,1)}) %reduce-scatter.19.cloned.1.call-update) | async-done | bytes 221200
  444.4 40.7 %all-reduce = (f32[768]{0:T(1024)}, f32[768]{0:T(1024)}, f32[768,8]{0,1:T(8,128)}) all-reduce(f32[768]{0:T(1024)S(1)} %get-tuple-element.51, f32[768]{0:T(1024)S(1)} %get-tuple-element.49, f32[768,8]{0,1:T(8,128)S(1)} %fusion.91), channel_id=1, replica_groups=mesh['fsdp'=4,'head'=4,'tensor'=2] {'fsdp','head','tensor'}, use_global_device_ids=true, to_apply=%region_23.24 | all-reduce | flops 7680 | bytes 61440 | tf_op jit(solution)/shard_map/psum | solution.py:191
  487.6 12.9 %reduce-scatter.15.cloned.1.call-done = bf16[2,192,1536]{2,1,0:T(8,128)(2,1)} async-done(((bf16[2,768,1536]{2,1,0:T(8,128)(2,1)}), bf16[2,192,1536]{2,1,0:T(8,128)(2,1)}) %reduce-scatter.15.cloned.1.call-update) | async-done | bytes 1179664 | tf_op jit(solution)/shard_map/reduce_scatter | solution.py:184
  503.4 56.9 %reduce-scatter.17.cloned.1.call-done = bf16[2,1536,192]{1,2,0:T(8,128)(2,1)} async-done(((bf16[2,1536,768]{1,2,0:T(8,128)(2,1)}), bf16[2,1536,192]{1,2,0:T(8,128)(2,1)}) %reduce-scatter.17.cloned.1.call-update) | async-done | bytes 1179664 | tf_op jit(solution)/shard_map/reduce_scatter | solution.py:184
  (195 shorter events, 108.0 us)
Async XLA Ops:
  8.0 37.7 %all-gather.4.cloned.1.call-start = ((), (), s32[]{:S(2)}) async-start(), calls=%async_computation.8 | async-start | bytes 1536000 | tf_op jit(solution)/shard_map/all_gather | solution.py:95
  11.7 73.4 %reduce-scatter.11.cloned.1.call-start = ((), (), s32[]{:S(2)}) async-start(), calls=%async_computation.9 | async-start | bytes 1536000 | tf_op jit(solution)/shard_map/reduce_scatter | solution.py:113
  55.5 32.0 %copy-start.28 = (f32[768]{0:T(1024)S(1)}, f32[768]{0:T(1024)}, u32[]{:S(2)}) copy-start(f32[768]{0:T(1024)} %param.16) | copy-start | bytes 9220
  55.5 33.1 %copy-start.29 = (bf16[768,8]{0,1:T(8,128)(2,1)S(1)}, bf16[768,8]{0,1:T(8,128)(2,1)}, u32[]{:S(2)}) copy-start(bf16[768,8]{0,1:T(8,128)(2,1)} %param.17) | copy-start | bytes 36868
  55.6 165.9 %all-gather.6.cloned.1.call-start = ((), (), s32[]{:S(2)}) async-start(), calls=%async_computation.10 | async-start | bytes 5898240 | tf_op jit(solution)/shard_map/all_gather | solution.py:96
  92.6 41.3 %all-to-all-start = ((bf16[4,2,64,1536]{3,2,1,0:T(8,128)(2,1)}), bf16[4,2,64,1536]{3,2,1,0:T(8,128)(2,1)}, u32[]{:S(2)}, u32[]{:S(2)}) async-start(bf16[4,2,64,1536]{3,2,1,0:T(8,128)(2,1)} %bitcast.259), calls=%async_computation.1 | async-start | bytes 3145728 | tf_op jit(solution)/shard_map/all_to_all | solution.py:134
  96.9 43.0 %collective-permute-start = (bf16[2,1536,192]{1,2,0:T(8,128)(2,1)}, bf16[2,1536,192]{1,2,0:T(8,128)(2,1)}, u32[]{:S(2)}, u32[]{:S(2)}) collective-permute-start(bf16[2,1536,192]{1,2,0:T(8,128)(2,1)} %param.19), channel_id=1, source_target_pairs={{0,8},{8,16},{16,24},{24,0},{1,9},{9,17},{17,25},{25,1},{2,10},{10... | collective-permute-start | bytes 3538952 | tf_op jit(solution)/shard_map/ppermute | solution.py:23
  136.5 81.1 %collective-permute-start.3 = (bf16[4,2,64,1536]{3,2,0,1:T(8,128)(2,1)}, bf16[4,2,64,1536]{3,2,0,1:T(8,128)(2,1)}, u32[]{:S(2)}, u32[]{:S(2)}) collective-permute-start(bf16[4,2,64,1536]{3,2,0,1:T(8,128)(2,1)} %copy.190), channel_id=1, source_target_pairs={{0,1},{1,0},{2,3},{3,2},{4,5},{5,4},{6,7},{7,6},{8,9},{9,8},{10,11... | collective-permute-start | bytes 4718600 | tf_op jit(solution)/shard_map/ppermute | solution.py:52
  136.5 43.5 %collective-permute-start.1 = (bf16[2,1536,192]{1,2,0:T(8,128)(2,1)}, bf16[2,1536,192]{1,2,0:T(8,128)(2,1)}, u32[]{:S(2)}, u32[]{:S(2)}) collective-permute-start(bf16[2,1536,192]{1,2,0:T(8,128)(2,1)} %param.19), channel_id=1, source_target_pairs={{0,24},{8,0},{16,8},{24,16},{1,25},{9,1},{17,9},{25,17},{2,26},{10... | collective-permute-start | bytes 3538952 | tf_op jit(solution)/shard_map/ppermute | solution.py:26
  139.9 59.9 %collective-permute-start.2 = (bf16[2,1536,192]{1,2,0:T(8,128)(2,1)}, bf16[2,1536,192]{1,2,0:T(8,128)(2,1)}, u32[]{:S(2)}, u32[]{:S(2)}) collective-permute-start(bf16[2,1536,192]{1,2,0:T(8,128)(2,1)} %collective-permute-done), channel_id=1, source_target_pairs={{0,8},{8,16},{16,24},{24,0},{1,9},{9,17},{17,25},{25,1},{2,10},{10... | collective-permute-start | bytes 3538952 | tf_op jit(solution)/shard_map/ppermute | solution.py:23
  260.5 3.5 collective-permute-start.4
  265.7 42.5 %all-to-all-start.1 = ((bf16[4,2,64,1536]{3,2,1,0:T(8,128)(2,1)}), bf16[4,2,64,1536]{3,2,1,0:T(8,128)(2,1)}, u32[]{:S(2)}, u32[]{:S(2)}) async-start(bf16[4,2,64,1536]{3,2,1,0:T(8,128)(2,1)} %copy.130), calls=%async_computation.2 | async-start | bytes 3145728 | tf_op jit(solution)/shard_map/all_to_all | solution.py:149
  270.8 74.4 %all-gather.8.cloned.1.call-start = ((), (), s32[]{:S(2)}) async-start(), calls=%async_computation.11 | async-start | bytes 1536000 | tf_op jit(solution)/shard_map/all_gather | solution.py:163
  314.5 69.5 %reduce-scatter.21.cloned.1.call-start = ((), (), s32[]{:S(2)}) async-start(), calls=%async_computation.16 | async-start | bytes 491520
  353.6 57.0 %reduce-scatter.13.cloned.1.call-start = ((), (), s32[]{:S(2)}) async-start(), calls=%async_computation.12 | async-start | bytes 1536000 | tf_op jit(solution)/shard_map/reduce_scatter | solution.py:176
  359.9 80.2 %reduce-scatter.19.cloned.1.call-start = ((), (), s32[]{:S(2)}) async-start(), calls=%async_computation.15 | async-start | bytes 1228800
  366.2 134.3 %reduce-scatter.15.cloned.1.call-start = ((), (), s32[]{:S(2)}) async-start(), calls=%async_computation.13 | async-start | bytes 5898240 | tf_op jit(solution)/shard_map/reduce_scatter | solution.py:184
  373.6 186.8 %reduce-scatter.17.cloned.1.call-start = ((), (), s32[]{:S(2)}) async-start(), calls=%async_computation.14 | async-start | bytes 5898240 | tf_op jit(solution)/shard_map/reduce_scatter | solution.py:184
  381.3 32.0 %copy-start.6 = (f32[1,197,768]{2,1,0:T(8,128)S(1)}, f32[1,197,768]{2,1,0:T(8,128)}, u32[]{:S(2)}) copy-start(f32[1,197,768]{2,1,0:T(8,128)} %copy-done.5) | copy-start | bytes 1815556
  382.3 1.6 collective-permute-start.5
  384.9 56.7 %collective-permute-start.8 = (bf16[192,192]{1,0:T(8,128)(2,1)S(1)}, bf16[192,192]{1,0:T(8,128)(2,1)}, u32[]{:S(2)}, u32[]{:S(2)}) collective-permute-start(bf16[192,192]{1,0:T(8,128)(2,1)S(1)} %copy.166), channel_id=1, source_target_pairs={{0,1},{1,0},{2,3},{3,2},{4,5},{5,4},{6,7},{7,6},{8,9},{9,8},{10,11... | collective-permute-start | bytes 221192 | tf_op jit(solution)/shard_map/ppermute | solution.py:52
  415.2 69.9 %collective-permute-start.6 = (f32[1,197,768]{2,0,1:T(1,128)S(1)}, f32[1,197,768]{2,0,1:T(1,128)S(1)}, u32[]{:S(2)}, u32[]{:S(2)}) collective-permute-start(f32[1,197,768]{2,0,1:T(1,128)S(1)} %copy.139), channel_id=1, source_target_pairs={{0,1},{1,0},{2,3},{3,2},{4,5},{5,4},{6,7},{7,6},{8,9},{9,8},{10,11... | collective-permute-start | bytes 1815560 | tf_op jit(solution)/shard_map/ppermute | solution.py:52
  441.5 1.7 collective-permute-start.7
  485.3 78.0 %copy-start.1 = (bf16[2,1,197,768]{3,0,2,1:T(2,128)(2,1)S(1)}, bf16[2,1,197,768]{3,0,2,1:T(2,128)(2,1)}, u32[]{:S(2)}) copy-start(bf16[2,1,197,768]{3,0,2,1:T(2,128)(2,1)} %param.12) | copy-start | bytes 1815556
  (30 other events, 122.0 us)
Sparse Core Ops, SparseCore 0:
  11.9 33.8 all-gather.3
  55.7 29.4 reduce-scatter.10
  314.6 30.5 all-gather.7
Sparse Core Ops, SparseCore 1:
  57.9 69.3 all-gather.5
  353.7 23.8 reduce-scatter.20
  380.4 30.2 reduce-scatter.12
  414.2 25.9 reduce-scatter.18
  443.2 57.3 reduce-scatter.14
  503.5 56.8 reduce-scatter.16
